TPU v7x, 32 devices: a whole 2x2x4 slice. The times are simulated.
32 devices in a mesh: blk: 2 (over core), pts: 4 (over y, x), bond: 4 (over z).
Axes of the slice: x: 2, y: 2, z: 4, core: 2. Of those that a mesh axis runs over, the one named last changes fastest.
Arguments:
- mps: bfloat16 [2, 1024, 2, 1024], P('blk', None, None, 'bond'), may hold values from -1 to 2, as said below
- couplings: float32 [64, 3], replicated, may hold values from 0.5 to 2
- point_ids: int32 [4], P('pts'), may hold values from 0 to 63
- site_group: int32 [2], P('blk'), may hold values from 0 to 7
- field_levels: float32 [8], replicated, may hold values from 0.3 to 3
- left_cut: float32 [1024, 1024], P('bond'), may hold values from -200 to 200, as said below
- right_cut: float32 [1024, 1024], P('bond'), may hold values from -200 to 200, as said below
Outputs:
- left_env: bfloat16 [2, 4, 5, 1024, 1024], P('blk', 'pts', None, 'bond')
- right_env: bfloat16 [2, 4, 5, 1024, 1024], P('blk', 'pts', None, 'bond')
- energies: float32 [4], P('pts')
Inputs may be any that keep to these rules, and one draw needn't show every extreme that they name: `mps`: each site tensor is the identity on spin 0 plus noise on both spins. `left_cut`: A symmetric matrix. `right_cut`: A symmetric matrix.
All inputs are finite; a program needn't handle non-finite values.
Results may differ from a plain program's by a relative error of at most 0.0066.
Values may be sent and summed in bfloat16 or wider, within the bound.
No kernel may reach another device: no remote copies, remote signals or barrier semaphores. Data moves between devices by JAX's collectives and lax.ppermute only.
A program may use at most 64 MiB of HBM per device.

v0:
```python
import jax
import jax.numpy as jnp
from jax import lax
from jax.sharding import PartitionSpec as P


def shortened(shard):
    return jax.tree.map(lambda a: a.astype(jnp.bfloat16) if a.dtype == jnp.float32 else a, shard)


def passed_along(value, axis, steps):
    count = lax.axis_size(axis)
    initial, last = (max(0, -steps), min(count, count - steps))
    return lax.ppermute(value, axis, [(source, source + steps) for source in range(initial, last)])


def mpo_table(coupling, field_term):
    identity = jnp.eye(2, dtype=jnp.float32)
    raising = jnp.array([[0.0, 1.0], [0.0, 0.0]], dtype=jnp.float32)
    lowering = jnp.array([[0.0, 0.0], [1.0, 0.0]], dtype=jnp.float32)
    diagonal_spin = jnp.array([[0.5, 0.0], [0.0, -0.5]], dtype=jnp.float32)
    zeros_block = jnp.zeros((2, 2), jnp.float32)
    half_xy = 0.5 * coupling[0]
    table_rows = [
        [identity, zeros_block, zeros_block, zeros_block, zeros_block],
        [raising, zeros_block, zeros_block, zeros_block, zeros_block],
        [lowering, zeros_block, zeros_block, zeros_block, zeros_block],
        [diagonal_spin, zeros_block, zeros_block, zeros_block, zeros_block],
        [
            coupling[2] * field_term * diagonal_spin,
            half_xy * lowering,
            half_xy * raising,
            coupling[1] * diagonal_spin,
            identity,
        ],
    ]
    return jnp.stack([jnp.stack(table_row) for table_row in table_rows])


def mirrored(environment):
    return jnp.stack(
        [environment[0], environment[2], environment[1], environment[3], environment[4]]
    )


def ket_forward(environment, tensor):
    return jnp.einsum(
        "wyx,xsz->wsyz", mirrored(environment), tensor, preferred_element_type=jnp.float32
    ).astype(jnp.bfloat16)


def ket_backward(environment, tensor):
    return jnp.einsum(
        "wyx,zsx->wsyz", mirrored(environment), tensor, preferred_element_type=jnp.float32
    ).astype(jnp.bfloat16)


def bra_forward(mixed_part, tensor):
    return jnp.einsum("vtyz,ytq->vzq", mixed_part, tensor, preferred_element_type=jnp.float32)


def bra_backward(mixed_part, tensor):
    return jnp.einsum("vtyz,qty->vzq", mixed_part, tensor, preferred_element_type=jnp.float32)


def mix_side(ket_part, weights):
    channel_count = ket_part.shape[0]
    spin_count = ket_part.shape[1]
    out_rows = []
    for out_channel in range(channel_count):
        spin_rows = []
        for out_spin in range(spin_count):
            total = jnp.zeros(ket_part.shape[2:], jnp.float32)
            for in_channel in range(channel_count):
                for in_spin in range(spin_count):
                    total = total + weights[in_channel, in_spin, out_spin, out_channel] * ket_part[
                        in_channel, in_spin
                    ].astype(jnp.float32)
            spin_rows.append(total.astype(jnp.bfloat16))
        out_rows.append(jnp.stack(spin_rows))
    return jnp.stack(out_rows)


def body(mps, couplings, point_ids, site_group, field_levels, left_cut, right_cut):
    blocks = lax.axis_size("blk")
    shards = lax.axis_size("bond")
    section = lax.axis_index("blk")
    middle = blocks // 2
    tensor = lax.all_gather(mps[0], "bond", axis=2, tiled=True)
    param_count = couplings.shape[0]
    choose_point = (point_ids[:, None] == jnp.arange(param_count, dtype=jnp.int32)[None, :]).astype(
        jnp.float32
    )
    params = jnp.dot(choose_point, couplings, precision=lax.Precision.HIGHEST)
    group_count = field_levels.shape[0]
    site_field = jnp.sum(
        jnp.where(site_group[0] == jnp.arange(group_count, dtype=jnp.int32), field_levels, 0.0)
    )
    tables = jax.vmap(lambda coupling: mpo_table(coupling, site_field))(params)
    left_weights = jnp.transpose(tables, (0, 1, 3, 4, 2))
    right_weights = jnp.transpose(tables, (0, 2, 3, 4, 1))
    row_count = left_cut.shape[0]
    column_count = left_cut.shape[1]
    empty_block = jnp.zeros((4, row_count, column_count), jnp.float32)
    left_start = jnp.concatenate([empty_block, left_cut[None]], 0).astype(jnp.bfloat16)
    right_start = jnp.concatenate([right_cut[None], empty_block], 0).astype(jnp.bfloat16)
    entry_count = left_start.shape[0] * row_count * column_count * shards
    points = point_ids.shape[0]
    buffer_zero = jnp.zeros((points,) + left_start.shape, jnp.bfloat16)

    def ket_any(environment, forward):
        return lax.cond(
            forward,
            lambda held: ket_forward(held, tensor),
            lambda held: ket_backward(held, tensor),
            environment,
        )

    def bra_any(mixed_part, forward):
        return lax.cond(
            forward,
            lambda held: bra_forward(held, tensor),
            lambda held: bra_backward(held, tensor),
            mixed_part,
        )

    def cross(kets, gauges, directions):
        mixes = tuple((mix_side(ket_part, gauge) for ket_part, gauge in zip(kets, gauges)))
        pieces = (
            lax.all_to_all(shortened(mixes[0]), "bond", split_axis=3, concat_axis=2, tiled=True),
        )
        fresh = tuple((bra_any(piece, forward) for piece, forward in zip(pieces, directions)))
        totals = lax.psum(tuple((jnp.sum(value * value) for value in fresh)), "bond")
        return tuple(
            (
                (value * lax.rsqrt(total / entry_count + 1e-06)).astype(jnp.bfloat16)
                for value, total in zip(fresh, totals)
            )
        )

    def relay(to_next, to_prev):
        from_prev = passed_along(to_next, "blk", 1)
        from_next = passed_along(to_prev, "blk", -1)
        return (from_prev, from_next)

    def single_turn(step_index, state_tuple):
        recv_left, recv_right, left_out, right_out, left_seen = state_tuple
        left_offset = step_index - section
        right_offset = step_index - (blocks - 1 - section)
        is_left = left_offset % 2 == 0
        left_point = left_offset // 2
        right_point = right_offset // 2
        left_slot = jnp.clip(left_point, 0, points - 1)
        right_slot = jnp.clip(right_point, 0, points - 1)
        left_in = jnp.where(section == 0, left_start, recv_left)
        right_in = jnp.where(section == blocks - 1, right_start, recv_right)
        env_in = jnp.where(is_left, left_in, right_in)
        gauge = jnp.where(is_left, left_weights[left_slot], right_weights[right_slot])
        ket_part = ket_any(env_in, is_left)
        (new_norm,) = cross((ket_part,), (gauge,), (is_left,))
        left_live = is_left & (left_point >= 0) & (left_point < points)
        right_live = jnp.logical_not(is_left) & (right_point >= 0) & (right_point < points)
        left_out = jnp.where(
            left_live, lax.dynamic_update_index_in_dim(left_out, new_norm, left_slot, 0), left_out
        )
        left_seen = jnp.where(
            left_live, lax.dynamic_update_index_in_dim(left_seen, left_in, left_slot, 0), left_seen
        )
        right_out = jnp.where(
            right_live,
            lax.dynamic_update_index_in_dim(right_out, new_norm, right_slot, 0),
            right_out,
        )
        recv_left, recv_right = relay(new_norm, new_norm)
        return (recv_left, recv_right, left_out, right_out, left_seen)

    initial_state = (left_start, right_start, buffer_zero, buffer_zero, buffer_zero)
    _, _, left_out, right_out, left_seen = lax.fori_loop(
        0, blocks + 2 * points - 2, single_turn, initial_state
    )
    seen_wide = left_seen.astype(jnp.float32)
    right_wide = right_out.astype(jnp.float32)
    numer = jnp.sum(seen_wide * right_wide, axis=(1, 2, 3))
    denom = jnp.sum(seen_wide[:, 4] * right_wide[:, 0], axis=(1, 2))
    at_middle = (section == middle).astype(jnp.float32)
    numer, denom = lax.psum((numer * at_middle, denom * at_middle), ("blk", "bond"))
    energies = numer / denom / blocks
    return (left_out[None], right_out[None], energies)


def solution(mesh):
    placed = (
        P("blk", None, None, "bond"),
        P(),
        P("pts"),
        P("blk"),
        P(),
        P("bond", None),
        P("bond", None),
    )
    return jax.shard_map(
        body,
        mesh=mesh,
        in_specs=placed,
        out_specs=(
            P("blk", "pts", None, "bond", None),
            P("blk", "pts", None, "bond", None),
            P("pts"),
        ),
        check_vma=False,
    )
```

profile of v0, /device:TPU:3, one launch (start us, length us, event | category | flops | bytes accessed | tf_op | source)
XLA Modules:
  0.0 679.1 jit_solution(7310853259697243009)
XLA Ops:
  21.6 70.1 %all-gather.3.cloned.1.call-done = bf16[1,1024,2,1024]{3,1,2,0:T(8,128)(2,1)} async-done(((bf16[1,1024,2,256]{3,1,2,0:T(8,128)(2,1)}), bf16[1,1024,2,1024]{3,1,2,0:T(8,128)(2,1)}) %all-gather.3.cloned.1.call-update) | async-done | bytes 4194320 | tf_op jit(solution)/shard_map/all_gather | solution.py:89
  91.7 548.1 %while.25 = (s32[]{:T(128)}, bf16[5,256,1024]{2,1,0:T(8,128)(2,1)}, bf16[5,256,1024]{2,1,0:T(8,128)(2,1)}, bf16[1,5,256,1024]{3,2,1,0:T(8,128)(2,1)}, bf16[1,5,2...) while((s32[]{:T(128)}, bf16[5,256,1024]{2,1,0:T(8,128)(2,1)}, ...), condition=%wide.region_8.9_spmd.clone, body=%wide.region_1.8_spmd.clone.sunk | while | flops 10856693760 | bytes 262147376 | solution.py:178
  96.0 3.9 bitcast_select_fusion.6
  100.7 6.5 conditional.9
  101.2 5.9 convert_bitcast_fusion
  107.2 7.4 %fusion.191 = bf16[1,256,1024]{2,1,0:T(8,128)(2,1)S(1)} fusion(f32[]{:T(128)} %bitcast.382, f32[]{:T(128)} %bitcast.383, f32[]{:T(128)} %bitcast.384, f32[]{:T(128)} %bitcast.385, f32[]{:T(128)} %bitcast.386, f32[]{:T(128)} %bitcast.387, f32[]{:T(128)} %bitcast.388, f32[]{:T(128)} %bitcast.389, f32[]{:T(128)} %bitcast.390, f32[]{:T(128)} %bitcast.391, ...), kind=kLoop, calls=%fused_computation.254.clone.1 | loop fusion | flops 7864320 | bytes 5767208 | tf_op jit(solution)/shard_map/while/body/eval_jaxpr/convert_element_type | solution.py:79
  114.6 7.6 %fusion.189 = bf16[1,256,1024]{2,1,0:T(8,128)(2,1)S(1)} fusion(f32[]{:T(128)} %bitcast.372, f32[]{:T(128)} %bitcast.373, f32[]{:T(128)} %bitcast.374, f32[]{:T(128)} %bitcast.375, f32[]{:T(128)} %bitcast.376, f32[]{:T(128)} %bitcast.377, f32[]{:T(128)} %bitcast.378, f32[]{:T(128)} %bitcast.379, f32[]{:T(128)} %bitcast.380, f32[]{:T(128)} %bitcast.381, ...), kind=kLoop, calls=%fused_computation.253.clone.1 | loop fusion | flops 7864320 | bytes 5767208 | tf_op jit(solution)/shard_map/while/body/eval_jaxpr/convert_element_type | solution.py:79
  123.3 7.5 %fusion.195 = bf16[1,256,1024]{2,1,0:T(8,128)(2,1)S(1)} fusion(f32[]{:T(128)} %bitcast.402, f32[]{:T(128)} %bitcast.403, f32[]{:T(128)} %bitcast.404, f32[]{:T(128)} %bitcast.405, f32[]{:T(128)} %bitcast.406, f32[]{:T(128)} %bitcast.407, f32[]{:T(128)} %bitcast.408, f32[]{:T(128)} %bitcast.409, f32[]{:T(128)} %bitcast.410, f32[]{:T(128)} %bitcast.411, ...), kind=kLoop, calls=%fused_computation.252.clone.1 | loop fusion | flops 7864320 | bytes 5767208 | tf_op jit(solution)/shard_map/while/body/eval_jaxpr/convert_element_type | solution.py:79
  130.8 7.5 %fusion.194 = bf16[1,256,1024]{2,1,0:T(8,128)(2,1)S(1)} fusion(f32[]{:T(128)} %bitcast.392, f32[]{:T(128)} %bitcast.393, f32[]{:T(128)} %bitcast.394, f32[]{:T(128)} %bitcast.395, f32[]{:T(128)} %bitcast.396, f32[]{:T(128)} %bitcast.397, f32[]{:T(128)} %bitcast.398, f32[]{:T(128)} %bitcast.399, f32[]{:T(128)} %bitcast.400, f32[]{:T(128)} %bitcast.401, ...), kind=kLoop, calls=%fused_computation.251.clone.1 | loop fusion | flops 7864320 | bytes 5767208 | tf_op jit(solution)/shard_map/while/body/eval_jaxpr/convert_element_type | solution.py:79
  139.3 7.6 %fusion.199 = bf16[1,256,1024]{2,1,0:T(8,128)(2,1)S(1)} fusion(f32[]{:T(128)} %bitcast.422, f32[]{:T(128)} %bitcast.423, f32[]{:T(128)} %bitcast.424, f32[]{:T(128)} %bitcast.425, f32[]{:T(128)} %bitcast.426, f32[]{:T(128)} %bitcast.427, f32[]{:T(128)} %bitcast.428, f32[]{:T(128)} %bitcast.429, f32[]{:T(128)} %bitcast.430, f32[]{:T(128)} %bitcast.431, ...), kind=kLoop, calls=%fused_computation.250.clone.1 | loop fusion | flops 7864320 | bytes 5767208 | tf_op jit(solution)/shard_map/while/body/eval_jaxpr/convert_element_type | solution.py:79
  146.9 7.6 %fusion.198 = bf16[1,256,1024]{2,1,0:T(8,128)(2,1)S(1)} fusion(f32[]{:T(128)} %bitcast.412, f32[]{:T(128)} %bitcast.413, f32[]{:T(128)} %bitcast.414, f32[]{:T(128)} %bitcast.415, f32[]{:T(128)} %bitcast.416, f32[]{:T(128)} %bitcast.417, f32[]{:T(128)} %bitcast.418, f32[]{:T(128)} %bitcast.419, f32[]{:T(128)} %bitcast.420, f32[]{:T(128)} %bitcast.421, ...), kind=kLoop, calls=%fused_computation.249.clone.1 | loop fusion | flops 7864320 | bytes 5767208 | tf_op jit(solution)/shard_map/while/body/eval_jaxpr/convert_element_type | solution.py:79
  155.5 7.5 %fusion.203 = bf16[1,256,1024]{2,1,0:T(8,128)(2,1)S(1)} fusion(f32[]{:T(128)} %bitcast.442, f32[]{:T(128)} %bitcast.443, f32[]{:T(128)} %bitcast.444, f32[]{:T(128)} %bitcast.445, f32[]{:T(128)} %bitcast.446, f32[]{:T(128)} %bitcast.447, f32[]{:T(128)} %bitcast.448, f32[]{:T(128)} %bitcast.449, f32[]{:T(128)} %bitcast.450, f32[]{:T(128)} %bitcast.451, ...), kind=kLoop, calls=%fused_computation.248.clone.1 | loop fusion | flops 7864320 | bytes 5767208 | tf_op jit(solution)/shard_map/while/body/eval_jaxpr/convert_element_type | solution.py:79
  163.0 7.4 %fusion.202 = bf16[1,256,1024]{2,1,0:T(8,128)(2,1)S(1)} fusion(f32[]{:T(128)} %bitcast.432, f32[]{:T(128)} %bitcast.433, f32[]{:T(128)} %bitcast.434, f32[]{:T(128)} %bitcast.435, f32[]{:T(128)} %bitcast.436, f32[]{:T(128)} %bitcast.437, f32[]{:T(128)} %bitcast.438, f32[]{:T(128)} %bitcast.439, f32[]{:T(128)} %bitcast.440, f32[]{:T(128)} %bitcast.441, ...), kind=kLoop, calls=%fused_computation.247.clone.1 | loop fusion | flops 7864320 | bytes 5767208 | tf_op jit(solution)/shard_map/while/body/eval_jaxpr/convert_element_type | solution.py:79
  171.4 7.4 %fusion.207 = bf16[1,256,1024]{2,1,0:T(8,128)(2,1)S(1)} fusion(f32[]{:T(128)} %bitcast.462, f32[]{:T(128)} %bitcast.463, f32[]{:T(128)} %bitcast.464, f32[]{:T(128)} %bitcast.465, f32[]{:T(128)} %bitcast.466, f32[]{:T(128)} %bitcast.467, f32[]{:T(128)} %bitcast.468, f32[]{:T(128)} %bitcast.469, f32[]{:T(128)} %bitcast.470, f32[]{:T(128)} %bitcast.471, ...), kind=kLoop, calls=%fused_computation.246.clone.1 | loop fusion | flops 7864320 | bytes 5767208 | tf_op jit(solution)/shard_map/while/body/eval_jaxpr/convert_element_type | solution.py:79
  178.8 7.5 %fusion.206 = bf16[1,256,1024]{2,1,0:T(8,128)(2,1)S(1)} fusion(f32[]{:T(128)} %bitcast.452, f32[]{:T(128)} %bitcast.453, f32[]{:T(128)} %bitcast.454, f32[]{:T(128)} %bitcast.455, f32[]{:T(128)} %bitcast.456, f32[]{:T(128)} %bitcast.457, f32[]{:T(128)} %bitcast.458, f32[]{:T(128)} %bitcast.459, f32[]{:T(128)} %bitcast.460, f32[]{:T(128)} %bitcast.461, ...), kind=kLoop, calls=%fused_computation.255.clone.1 | loop fusion | flops 7864320 | bytes 5767208 | tf_op jit(solution)/shard_map/while/body/eval_jaxpr/convert_element_type | solution.py:79
  187.4 13.7 %copy.73 = bf16[5,2,256,1024]{2,1,0,3:T(2,128)(2,1)} copy(bf16[5,2,256,1024]{3,2,1,0:T(8,128)(2,1)} %fusion.208) | data formatting | bytes 10485760 | tf_op jit(solution)/shard_map/while/body/eval_jaxpr/stack | solution.py:81
  201.1 5.1 all-to-all-start
  206.2 115.2 %all-to-all-done = bf16[5,2,256,1024]{2,1,0,3:T(2,128)(2,1)} async-done(((bf16[5,2,256,1024]{2,1,0,3:T(2,128)(2,1)}), bf16[5,2,256,1024]{2,1,0,3:T(2,128)(2,1)}, u32[]{:S(2)}, u32[]{:S(2)}) %all-to-all-start) | async-done | bytes 5242912 | tf_op jit(solution)/shard_map/while/body/eval_jaxpr/all_to_all | solution.py:130
  325.1 8.1 %conditional.10 = (f32[5,256,1024]{2,1,0:T(8,128)}) conditional(s32[]{:T(128)} %convert_element_type.1877, (bf16[5,2,4,256,256]{3,4,2,1,0:T(8,128)(2,1)S(1)}, bf16[1024,2,1024]{2,0,1:T(8,128)(2,1)S(1)}) %tuple.251, (bf16[5,2,4,256,256]{3,4,2,1,0:T(8,128)(2,1)S(1)}, bf16[1024,2,1024]{2,0,1:T(8,128)(2,1)S(1)}) %tuple.252), branch_computations={%region_4.4_spmd, %region_5.5_spmd} | conditional | flops 5368709120 | bytes 25165832 | solution.py:120
  325.8 7.4 %fusion.24 = f32[5,256,1024]{2,1,0:T(8,128)} fusion(bf16[5,2,1024,256]{2,3,1,0:T(8,128)(2,1)S(1)} %bitcast.479, bf16[1024,2,1024]{2,0,1:T(8,128)(2,1)S(1)} %get-tuple-element.542), kind=kOutput, calls=%fused_computation.26 | convolution fusion | flops 5368709120 | bytes 14680064 | tf_op jit(solution)/shard_map/while/body/eval_jaxpr/cond/branch_0_fun/vtyz,qty->vzq/dot_general | solution.py:63
  333.2 4.5 multiply_reduce_fusion.3
  337.7 7.3 %psum.33 = f32[]{:T(128)} all-reduce(f32[]{:T(128)} %multiply_reduce_fusion.3), channel_id=1, replica_groups=mesh['blk'=2,'pts'=4,'bond'=4] {'bond'}, use_global_device_ids=true, to_apply=%region_7.7 | all-reduce | flops 1 | bytes 8 | tf_op jit(solution)/shard_map/while/body/eval_jaxpr/psum | solution.py:133
  345.8 4.4 bitcast_select_fusion.7
  350.2 7.9 %collective-permute-start.1 = (bf16[5,256,1024]{2,1,0:T(8,128)(2,1)S(1)}, bf16[5,256,1024]{2,1,0:T(8,128)(2,1)}, u32[]{:S(2)}, u32[]{:S(2)}) collective-permute-start(bf16[5,256,1024]{2,1,0:T(8,128)(2,1)S(1)} %get-tuple-element.1151), channel_id=1, source_target_pairs={{16,0},{17,1},{18,2},{19,3},{20,4},{21,5},{22,6},{23,7},{24,8},{25... | collective-permute-start | bytes 7864328 | tf_op jit(solution)/shard_map/while/body/eval_jaxpr/ppermute | solution.py:14
  369.2 4.6 bitcast_select_fusion.6
  374.7 6.4 conditional.9
  375.2 5.9 convert_bitcast_fusion.1
  381.1 7.4 %fusion.191 = bf16[1,256,1024]{2,1,0:T(8,128)(2,1)S(1)} fusion(f32[]{:T(128)} %bitcast.382, f32[]{:T(128)} %bitcast.383, f32[]{:T(128)} %bitcast.384, f32[]{:T(128)} %bitcast.385, f32[]{:T(128)} %bitcast.386, f32[]{:T(128)} %bitcast.387, f32[]{:T(128)} %bitcast.388, f32[]{:T(128)} %bitcast.389, f32[]{:T(128)} %bitcast.390, f32[]{:T(128)} %bitcast.391, ...), kind=kLoop, calls=%fused_computation.254.clone.1 | loop fusion | flops 7864320 | bytes 5767208 | tf_op jit(solution)/shard_map/while/body/eval_jaxpr/convert_element_type | solution.py:79
  388.5 7.6 %fusion.189 = bf16[1,256,1024]{2,1,0:T(8,128)(2,1)S(1)} fusion(f32[]{:T(128)} %bitcast.372, f32[]{:T(128)} %bitcast.373, f32[]{:T(128)} %bitcast.374, f32[]{:T(128)} %bitcast.375, f32[]{:T(128)} %bitcast.376, f32[]{:T(128)} %bitcast.377, f32[]{:T(128)} %bitcast.378, f32[]{:T(128)} %bitcast.379, f32[]{:T(128)} %bitcast.380, f32[]{:T(128)} %bitcast.381, ...), kind=kLoop, calls=%fused_computation.253.clone.1 | loop fusion | flops 7864320 | bytes 5767208 | tf_op jit(solution)/shard_map/while/body/eval_jaxpr/convert_element_type | solution.py:79
  397.2 7.5 %fusion.195 = bf16[1,256,1024]{2,1,0:T(8,128)(2,1)S(1)} fusion(f32[]{:T(128)} %bitcast.402, f32[]{:T(128)} %bitcast.403, f32[]{:T(128)} %bitcast.404, f32[]{:T(128)} %bitcast.405, f32[]{:T(128)} %bitcast.406, f32[]{:T(128)} %bitcast.407, f32[]{:T(128)} %bitcast.408, f32[]{:T(128)} %bitcast.409, f32[]{:T(128)} %bitcast.410, f32[]{:T(128)} %bitcast.411, ...), kind=kLoop, calls=%fused_computation.252.clone.1 | loop fusion | flops 7864320 | bytes 5767208 | tf_op jit(solution)/shard_map/while/body/eval_jaxpr/convert_element_type | solution.py:79
  404.7 7.5 %fusion.194 = bf16[1,256,1024]{2,1,0:T(8,128)(2,1)S(1)} fusion(f32[]{:T(128)} %bitcast.392, f32[]{:T(128)} %bitcast.393, f32[]{:T(128)} %bitcast.394, f32[]{:T(128)} %bitcast.395, f32[]{:T(128)} %bitcast.396, f32[]{:T(128)} %bitcast.397, f32[]{:T(128)} %bitcast.398, f32[]{:T(128)} %bitcast.399, f32[]{:T(128)} %bitcast.400, f32[]{:T(128)} %bitcast.401, ...), kind=kLoop, calls=%fused_computation.251.clone.1 | loop fusion | flops 7864320 | bytes 5767208 | tf_op jit(solution)/shard_map/while/body/eval_jaxpr/convert_element_type | solution.py:79
  413.2 7.6 %fusion.199 = bf16[1,256,1024]{2,1,0:T(8,128)(2,1)S(1)} fusion(f32[]{:T(128)} %bitcast.422, f32[]{:T(128)} %bitcast.423, f32[]{:T(128)} %bitcast.424, f32[]{:T(128)} %bitcast.425, f32[]{:T(128)} %bitcast.426, f32[]{:T(128)} %bitcast.427, f32[]{:T(128)} %bitcast.428, f32[]{:T(128)} %bitcast.429, f32[]{:T(128)} %bitcast.430, f32[]{:T(128)} %bitcast.431, ...), kind=kLoop, calls=%fused_computation.250.clone.1 | loop fusion | flops 7864320 | bytes 5767208 | tf_op jit(solution)/shard_map/while/body/eval_jaxpr/convert_element_type | solution.py:79
  420.8 7.6 %fusion.198 = bf16[1,256,1024]{2,1,0:T(8,128)(2,1)S(1)} fusion(f32[]{:T(128)} %bitcast.412, f32[]{:T(128)} %bitcast.413, f32[]{:T(128)} %bitcast.414, f32[]{:T(128)} %bitcast.415, f32[]{:T(128)} %bitcast.416, f32[]{:T(128)} %bitcast.417, f32[]{:T(128)} %bitcast.418, f32[]{:T(128)} %bitcast.419, f32[]{:T(128)} %bitcast.420, f32[]{:T(128)} %bitcast.421, ...), kind=kLoop, calls=%fused_computation.249.clone.1 | loop fusion | flops 7864320 | bytes 5767208 | tf_op jit(solution)/shard_map/while/body/eval_jaxpr/convert_element_type | solution.py:79
  429.5 7.5 %fusion.203 = bf16[1,256,1024]{2,1,0:T(8,128)(2,1)S(1)} fusion(f32[]{:T(128)} %bitcast.442, f32[]{:T(128)} %bitcast.443, f32[]{:T(128)} %bitcast.444, f32[]{:T(128)} %bitcast.445, f32[]{:T(128)} %bitcast.446, f32[]{:T(128)} %bitcast.447, f32[]{:T(128)} %bitcast.448, f32[]{:T(128)} %bitcast.449, f32[]{:T(128)} %bitcast.450, f32[]{:T(128)} %bitcast.451, ...), kind=kLoop, calls=%fused_computation.248.clone.1 | loop fusion | flops 7864320 | bytes 5767208 | tf_op jit(solution)/shard_map/while/body/eval_jaxpr/convert_element_type | solution.py:79
  436.9 7.4 %fusion.202 = bf16[1,256,1024]{2,1,0:T(8,128)(2,1)S(1)} fusion(f32[]{:T(128)} %bitcast.432, f32[]{:T(128)} %bitcast.433, f32[]{:T(128)} %bitcast.434, f32[]{:T(128)} %bitcast.435, f32[]{:T(128)} %bitcast.436, f32[]{:T(128)} %bitcast.437, f32[]{:T(128)} %bitcast.438, f32[]{:T(128)} %bitcast.439, f32[]{:T(128)} %bitcast.440, f32[]{:T(128)} %bitcast.441, ...), kind=kLoop, calls=%fused_computation.247.clone.1 | loop fusion | flops 7864320 | bytes 5767208 | tf_op jit(solution)/shard_map/while/body/eval_jaxpr/convert_element_type | solution.py:79
  445.3 7.4 %fusion.207 = bf16[1,256,1024]{2,1,0:T(8,128)(2,1)S(1)} fusion(f32[]{:T(128)} %bitcast.462, f32[]{:T(128)} %bitcast.463, f32[]{:T(128)} %bitcast.464, f32[]{:T(128)} %bitcast.465, f32[]{:T(128)} %bitcast.466, f32[]{:T(128)} %bitcast.467, f32[]{:T(128)} %bitcast.468, f32[]{:T(128)} %bitcast.469, f32[]{:T(128)} %bitcast.470, f32[]{:T(128)} %bitcast.471, ...), kind=kLoop, calls=%fused_computation.246.clone.1 | loop fusion | flops 7864320 | bytes 5767208 | tf_op jit(solution)/shard_map/while/body/eval_jaxpr/convert_element_type | solution.py:79
  452.7 7.5 %fusion.206 = bf16[1,256,1024]{2,1,0:T(8,128)(2,1)S(1)} fusion(f32[]{:T(128)} %bitcast.452, f32[]{:T(128)} %bitcast.453, f32[]{:T(128)} %bitcast.454, f32[]{:T(128)} %bitcast.455, f32[]{:T(128)} %bitcast.456, f32[]{:T(128)} %bitcast.457, f32[]{:T(128)} %bitcast.458, f32[]{:T(128)} %bitcast.459, f32[]{:T(128)} %bitcast.460, f32[]{:T(128)} %bitcast.461, ...), kind=kLoop, calls=%fused_computation.255.clone.1 | loop fusion | flops 7864320 | bytes 5767208 | tf_op jit(solution)/shard_map/while/body/eval_jaxpr/convert_element_type | solution.py:79
  461.4 13.7 %copy.73 = bf16[5,2,256,1024]{2,1,0,3:T(2,128)(2,1)} copy(bf16[5,2,256,1024]{3,2,1,0:T(8,128)(2,1)} %fusion.208) | data formatting | bytes 10485760 | tf_op jit(solution)/shard_map/while/body/eval_jaxpr/stack | solution.py:81
  475.0 5.1 all-to-all-start
  480.1 115.2 %all-to-all-done = bf16[5,2,256,1024]{2,1,0,3:T(2,128)(2,1)} async-done(((bf16[5,2,256,1024]{2,1,0,3:T(2,128)(2,1)}), bf16[5,2,256,1024]{2,1,0,3:T(2,128)(2,1)}, u32[]{:S(2)}, u32[]{:S(2)}) %all-to-all-start) | async-done | bytes 5242912 | tf_op jit(solution)/shard_map/while/body/eval_jaxpr/all_to_all | solution.py:130
  599.0 8.0 %conditional.10 = (f32[5,256,1024]{2,1,0:T(8,128)}) conditional(s32[]{:T(128)} %convert_element_type.1877, (bf16[5,2,4,256,256]{3,4,2,1,0:T(8,128)(2,1)S(1)}, bf16[1024,2,1024]{2,0,1:T(8,128)(2,1)S(1)}) %tuple.251, (bf16[5,2,4,256,256]{3,4,2,1,0:T(8,128)(2,1)S(1)}, bf16[1024,2,1024]{2,0,1:T(8,128)(2,1)S(1)}) %tuple.252), branch_computations={%region_4.4_spmd, %region_5.5_spmd} | conditional | flops 5368709120 | bytes 25165832 | solution.py:120
  599.8 7.2 %fusion.29 = f32[5,256,1024]{2,1,0:T(8,128)} fusion(bf16[5,2,1024,256]{2,3,1,0:T(8,128)(2,1)S(1)} %bitcast.480, bf16[1024,2,1024]{2,0,1:T(8,128)(2,1)S(1)} %get-tuple-element.544), kind=kOutput, calls=%fused_computation.29 | convolution fusion | flops 5368709120 | bytes 14680064 | tf_op jit(solution)/shard_map/while/body/eval_jaxpr/cond/branch_1_fun/vtyz,ytq->vzq/dot_general | solution.py:59
  607.0 4.5 multiply_reduce_fusion.3
  611.5 7.3 %psum.33 = f32[]{:T(128)} all-reduce(f32[]{:T(128)} %multiply_reduce_fusion.3), channel_id=1, replica_groups=mesh['blk'=2,'pts'=4,'bond'=4] {'bond'}, use_global_device_ids=true, to_apply=%region_7.7 | all-reduce | flops 1 | bytes 8 | tf_op jit(solution)/shard_map/while/body/eval_jaxpr/psum | solution.py:133
  619.5 5.2 bitcast_select_fusion.7
  624.7 8.2 %collective-permute-start.1 = (bf16[5,256,1024]{2,1,0:T(8,128)(2,1)S(1)}, bf16[5,256,1024]{2,1,0:T(8,128)(2,1)}, u32[]{:S(2)}, u32[]{:S(2)}) collective-permute-start(bf16[5,256,1024]{2,1,0:T(8,128)(2,1)S(1)} %get-tuple-element.1151), channel_id=1, source_target_pairs={{16,0},{17,1},{18,2},{19,3},{20,4},{21,5},{22,6},{23,7},{24,8},{25... | collective-permute-start | bytes 7864328 | tf_op jit(solution)/shard_map/while/body/eval_jaxpr/ppermute | solution.py:14
  639.9 4.9 convert_element_type.895
  653.6 16.1 %all-reduce.6 = (f32[1]{0:T(128)}, f32[1]{0:T(128)}) all-reduce(f32[1]{0:T(128)} %bitcast.36, f32[1]{0:T(128)} %bitcast.37), channel_id=1, replica_groups=mesh['blk'=2,'pts'=4,'bond'=4] {'blk','bond'}, use_global_device_ids=true, to_apply=%region_10.11 | all-reduce | flops 2 | bytes 16 | tf_op jit(solution)/shard_map/psum | solution.py:186
  (117 shorter events, 62.8 us)
Async XLA Ops:
  7.2 4.7 copy-start
  7.2 6.8 copy-start.14
  7.2 8.2 %copy-start.12 = (f32[2,2]{1,0:T(2,128)S(1)}, f32[2,2]{1,0:T(2,128)}, u32[]{:S(2)}) copy-start(f32[2,2]{1,0:T(2,128)} %constant.163.clone) | copy-start | bytes 52
  7.2 8.2 %copy-start.13 = (f32[2,2]{1,0:T(2,128)S(1)}, f32[2,2]{1,0:T(2,128)}, u32[]{:S(2)}) copy-start(f32[2,2]{1,0:T(2,128)} %constant.162.clone) | copy-start | bytes 52
  7.2 8.6 %copy-start.11 = (f32[1,1,5,2,2]{2,4,3,1,0:T(2,128)S(1)}, f32[1,1,5,2,2]{2,4,3,1,0:T(2,128)}, u32[]{:S(2)}) copy-start(f32[1,1,5,2,2]{2,4,3,1,0:T(2,128)} %constant.182) | copy-start | bytes 244
  7.2 8.6 %copy-start.10 = (f32[1,1,5,2,2]{2,4,3,1,0:T(2,128)S(1)}, f32[1,1,5,2,2]{2,4,3,1,0:T(2,128)}, u32[]{:S(2)}) copy-start(f32[1,1,5,2,2]{2,4,3,1,0:T(2,128)} %constant.185) | copy-start | bytes 244
  7.2 8.6 %copy-start.9 = (f32[1,1,5,2,2]{2,4,3,1,0:T(2,128)S(1)}, f32[1,1,5,2,2]{2,4,3,1,0:T(2,128)}, u32[]{:S(2)}) copy-start(f32[1,1,5,2,2]{2,4,3,1,0:T(2,128)} %constant.188) | copy-start | bytes 244
  7.3 3.9 copy-start.17
  7.3 8.8 %copy-start.7 = (f32[256,1024]{1,0:T(8,128)S(1)}, f32[256,1024]{1,0:T(8,128)}, u32[]{:S(2)}) copy-start(f32[256,1024]{1,0:T(8,128)} %param.22) | copy-start | bytes 3145732
  7.3 84.5 %all-gather.3.cloned.1.call-start = ((), (), s32[]{:S(2)}) async-start(), calls=%async_computation.1 | async-start | bytes 5242880 | tf_op jit(solution)/shard_map/all_gather | solution.py:89
  9.8 6.7 copy-start.8
  16.4 3.7 copy-start.2
  16.8 1.7 copy-start.4
  95.9 3.9 copy-start.3
  96.0 4.7 copy-start.15
  201.1 120.3 %all-to-all-start = ((bf16[5,2,256,1024]{2,1,0,3:T(2,128)(2,1)}), bf16[5,2,256,1024]{2,1,0,3:T(2,128)(2,1)}, u32[]{:S(2)}, u32[]{:S(2)}) async-start(bf16[5,2,256,1024]{2,1,0,3:T(2,128)(2,1)} %copy.73), calls=%async_computation | async-start | bytes 10485760 | tf_op jit(solution)/shard_map/while/body/eval_jaxpr/all_to_all | solution.py:130
  321.4 3.7 copy-start.16
  350.2 11.0 %collective-permute-start.1 = (bf16[5,256,1024]{2,1,0:T(8,128)(2,1)S(1)}, bf16[5,256,1024]{2,1,0:T(8,128)(2,1)}, u32[]{:S(2)}, u32[]{:S(2)}) collective-permute-start(bf16[5,256,1024]{2,1,0:T(8,128)(2,1)S(1)} %get-tuple-element.1151), channel_id=1, source_target_pairs={{16,0},{17,1},{18,2},{19,3},{20,4},{21,5},{22,6},{23,7},{24,8},{25... | collective-permute-start | bytes 7864328 | tf_op jit(solution)/shard_map/while/body/eval_jaxpr/ppermute | solution.py:14
  358.1 6.9 %collective-permute-start = (bf16[5,256,1024]{2,1,0:T(8,128)(2,1)S(1)}, bf16[5,256,1024]{2,1,0:T(8,128)(2,1)}, u32[]{:S(2)}, u32[]{:S(2)}) collective-permute-start(bf16[5,256,1024]{2,1,0:T(8,128)(2,1)S(1)} %get-tuple-element.1151), channel_id=1, source_target_pairs={{0,16},{1,17},{2,18},{3,19},{4,20},{5,21},{6,22},{7,23},{8,24},{9,... | collective-permute-start | bytes 7864328 | tf_op jit(solution)/shard_map/while/body/eval_jaxpr/ppermute | solution.py:14
  369.2 4.7 copy-start.3
  369.2 5.5 copy-start.15
  475.0 120.3 %all-to-all-start = ((bf16[5,2,256,1024]{2,1,0,3:T(2,128)(2,1)}), bf16[5,2,256,1024]{2,1,0,3:T(2,128)(2,1)}, u32[]{:S(2)}, u32[]{:S(2)}) async-start(bf16[5,2,256,1024]{2,1,0,3:T(2,128)(2,1)} %copy.73), calls=%async_computation | async-start | bytes 10485760 | tf_op jit(solution)/shard_map/while/body/eval_jaxpr/all_to_all | solution.py:130
  595.3 3.7 copy-start.16
  624.7 13.0 %collective-permute-start.1 = (bf16[5,256,1024]{2,1,0:T(8,128)(2,1)S(1)}, bf16[5,256,1024]{2,1,0:T(8,128)(2,1)}, u32[]{:S(2)}, u32[]{:S(2)}) collective-permute-start(bf16[5,256,1024]{2,1,0:T(8,128)(2,1)S(1)} %get-tuple-element.1151), channel_id=1, source_target_pairs={{16,0},{17,1},{18,2},{19,3},{20,4},{21,5},{22,6},{23,7},{24,8},{25... | collective-permute-start | bytes 7864328 | tf_op jit(solution)/shard_map/while/body/eval_jaxpr/ppermute | solution.py:14
  633.0 6.9 %collective-permute-start = (bf16[5,256,1024]{2,1,0:T(8,128)(2,1)S(1)}, bf16[5,256,1024]{2,1,0:T(8,128)(2,1)}, u32[]{:S(2)}, u32[]{:S(2)}) collective-permute-start(bf16[5,256,1024]{2,1,0:T(8,128)(2,1)S(1)} %get-tuple-element.1151), channel_id=1, source_target_pairs={{0,16},{1,17},{2,18},{3,19},{4,20},{5,21},{6,22},{7,23},{8,24},{9,... | collective-permute-start | bytes 7864328 | tf_op jit(solution)/shard_map/while/body/eval_jaxpr/ppermute | solution.py:14
  639.9 4.9 copy-start.5
  639.9 4.9 copy-start.6
  646.9 24.1 %copy-start.1 = (f32[64,3]{0,1:T(4,128)S(1)}, f32[64,3]{0,1:T(4,128)}, u32[]{:S(2)}) copy-start(f32[64,3]{0,1:T(4,128)} %param.17) | copy-start | bytes 2308
Sparse Core Ops, SparseCore 0:
  9.9 81.8 all-gather.2
where the time goes:
time: 682 us; the launch traced here: 679 us
  waiting for transfers between devices  306 us (45%)
  other arithmetic  208 us (30%)
  local copies, waits for them, and re-layouts  55.8 us (8%)
  blocking collectives  30.8 us (5%)
  starting transfers between devices  28.8 us (4%)
  matrix products  26.6 us (4%)
  between operations  21.4 us (3%)
    all_to_all x2, waiting for transfers between devices, cross(): lax.all_to_all(shortened(mixes[0]), 'bond', split_axis=3, concat_axis=2,...  230 us
    convert_element_type x20, other arithmetic, mix_side(): spin_rows.append(total.astype(jnp.bfloat16))  150 us
    all_gather x1, waiting for transfers between devices, body(): tensor = lax.all_gather(mps[0], 'bond', axis=2, tiled=True)  70.1 us
    another operation x2, local copies, waits for them, and re-layouts, mix_side(): return jnp.stack(out_rows)  27.3 us
    ppermute x4, starting transfers between devices, passed_along(): lax.ppermute(value, axis, [(source, source + steps) for source in range(i...  18.6 us
    psum x1, blocking collectives, body(): lax.psum((numer * at_middle, denom * at_middle), ('blk', 'bond'))  16.1 us
    psum x2, blocking collectives, cross(): lax.psum(tuple((jnp.sum(value * value) for value in fresh)), 'bond')  14.6 us
  transfers between devices with their start and end apart: 7, of which 5 were waited for; matrix products, arithmetic and copies ran while one was open for 2% of the time, Pallas kernels for 0%

commit v1 on v0

v1 whole, which is shorter than its diff:
```python
import functools

import jax
import jax.numpy as jnp
from jax import lax
from jax.experimental import pallas as pl
from jax.experimental.pallas import tpu as pltpu
from jax.sharding import PartitionSpec as P

F32 = jnp.float32
BF16 = jnp.bfloat16
EPS = 1e-06
SHRINK = 2.0**-8


def dot_nn(lhs, rhs):
    return lax.dot_general(lhs, rhs, (((1,), (0,)), ((), ())), preferred_element_type=F32)


def dot_nt(lhs, rhs):
    return lax.dot_general(lhs, rhs, (((1,), (1,)), ((), ())), preferred_element_type=F32)


def shifted(value, axis, step):
    count = lax.axis_size(axis)
    return lax.ppermute(value, axis, [(i, (i + step) % count) for i in range(count)])


def crossed(value, axis, mask):
    count = lax.axis_size(axis)
    return lax.ppermute(value, axis, [(i, i ^ mask) for i in range(count)])


def swapped(value):
    return shifted(value, "blk", 1)


def power_of_two(count):
    return count & (count - 1) == 0


def bond_total(value):
    count = lax.axis_size("bond")
    if count == 1:
        return value
    if not power_of_two(count) or count > 8:
        return lax.psum(value, "bond")
    parts = [value] + [crossed(value, "bond", mask) for mask in range(1, count)]
    while len(parts) > 1:
        parts = [parts[i] + parts[i + 1] for i in range(0, len(parts), 2)]
    return parts[0]


def gather_pieces(tensor, cut):
    points = lax.axis_size("pts")
    shards = lax.axis_size("bond")
    chi = tensor.shape[1]
    width = tensor.shape[2]
    part = chi // points
    packs = [
        jnp.concatenate(
            [
                tensor[:, q * part : (q + 1) * part, :].reshape(2 * part, width),
                cut[:, q * part : (q + 1) * part],
            ]
        )
        for q in range(points)
    ]
    here = lax.axis_index("pts")
    mine = lax.dynamic_index_in_dim(jnp.stack(packs), here, 0, keepdims=False)
    found = []
    for step in range(1, shards):
        came = shifted(mine, "bond", step)
        found.append((came, step, 0))
        for mask in range(1, points):
            found.append((crossed(came, "pts", mask), step, mask))
    local = [(packs[q], 0, q) for q in range(points)]
    return local, found


def energy_kernel(shape, plan, scal, ints, xt_ref, *refs):
    chi, width, part, points, shards = shape
    count = len(plan)
    sources = refs[:count]
    raw, sums = refs[count : count + 2]
    own, oth, own_cut, oth_cut, xa, xb, va, t1, t2, yg, sems = refs[count + 2 :]
    core, here, spot = ints[0], ints[1], ints[2]
    tile = 256 if chi % 256 == 0 else chi
    tiles = chi // tile

    copies = []
    for index, (source, (is_other, step, mask, local)) in enumerate(zip(sources, plan)):
        site = oth if is_other else own
        site_cut = oth_cut if is_other else own_cut
        if step is None:
            copies.append((source, site if mask == 0 else site_cut))
            continue
        shard = lax.rem(spot + shards - step, shards)
        quarter = mask if local else lax.bitwise_xor(here, mask)
        rows = pl.ds(pl.multiple_of(quarter * part, part), part)
        cols = pl.ds(pl.multiple_of(shard * width, width), width)
        copies.append((source.at[pl.ds(0, part)], site.at[0, rows, cols]))
        copies.append((source.at[pl.ds(part, part)], site.at[1, rows, cols]))
        cut_rows = pl.ds(pl.multiple_of(shard * width, width), width)
        cut_cols = pl.ds(pl.multiple_of(quarter * part, part), part)
        copies.append((source.at[pl.ds(2 * part, width)], site_cut.at[cut_rows, cut_cols]))
    started = []
    for index, (source, target) in enumerate(copies):
        copy = pltpu.make_async_copy(source, target, sems.at[index])
        copy.start()
        started.append(copy)
    for copy in started:
        copy.wait()

    mine = pl.ds(pl.multiple_of(spot * width, width), width)

    def run(first, last, xs_first_transposed):
        def cols_of(ref, index, form, at):
            return ref[index, :, at] if form is dot_nn else ref[index, at, :]

        x_first, x_second = xa, xb
        for s in range(2):
            rows = pl.ds(s * width, width)
            if xs_first_transposed:
                x_first[rows, :] = xt_ref[s]
                x_second[rows, :] = own[s, mine, :]
            else:
                x_first[rows, :] = own[s, mine, :]
                x_second[rows, :] = xt_ref[s]

        def cut_first(j, carry):
            at = pl.ds(pl.multiple_of(j * tile, tile), tile)
            va[:, at] = dot_nn(x_first[...], own_cut[:, at]).astype(BF16)
            return carry

        lax.fori_loop(0, tiles, cut_first, 0)

        def stage_one(j, carry):
            at = pl.ds(pl.multiple_of(j * tile, tile), tile)
            up = first(va[...], cols_of(own, 0, first, at))
            down = first(va[...], cols_of(own, 1, first, at))
            p00, p10 = up[:width], up[width:]
            p01, p11 = down[:width], down[width:]
            plus, minus = p00 + p11, p00 - p11
            raw[0, :, at] = plus
            raw[1, :, at] = minus
            raw[2, :, at] = p01
            raw[3, :, at] = p10
            return tuple(c + jnp.sum(v * v) for c, v in zip(carry, (plus, minus, p01, p10)))

        zero = jnp.zeros((), F32)
        s_plus, s_minus, s_01, s_10 = lax.fori_loop(0, tiles, stage_one, (zero,) * 4)
        sums[0] = s_plus
        sums[1] = s_minus
        sums[2] = s_01 + s_10

        def first_product(j, carry):
            at = pl.ds(pl.multiple_of(j * tile, tile), tile)
            for t in range(2):
                rows = pl.ds(t * 2 * width, 2 * width)
                t1[rows, at] = first(x_second[...], cols_of(oth, t, first, at)).astype(BF16)
            return carry

        lax.fori_loop(0, tiles, first_product, 0)

        def cut_second(j, carry):
            at = pl.ds(pl.multiple_of(j * tile, tile), tile)
            t2[:, at] = dot_nn(t1[...], oth_cut[:, at]).astype(BF16)
            return carry

        lax.fori_loop(0, tiles, cut_second, 0)

        plus_scale, minus_scale, xy_scale, field_scale = scal[0], scal[1], scal[2], scal[3]

        def mixing(j, carry):
            at = pl.ds(pl.multiple_of(j * tile, tile), tile)
            q0 = last(t2[: 3 * width], cols_of(oth, 0, last, at))
            q1 = last(t2[width:], cols_of(oth, 1, last, at))
            a0, a1, a01 = q0[:width], q0[width : 2 * width], q0[2 * width :]
            b10, b0, b1 = q1[:width], q1[width : 2 * width], q1[2 * width :]
            sum0, sum1 = a0 + b0, a1 + b1
            y0 = plus_scale * (a0 - b0) + xy_scale * b10 + field_scale * sum0
            y1 = minus_scale * (a1 - b1) + xy_scale * a01 - field_scale * sum1
            yg[pl.ds(0, width), at] = y0.astype(BF16)
            yg[pl.ds(width, width), at] = sum0.astype(BF16)
            yg[pl.ds(2 * width, width), at] = sum1.astype(BF16)
            yg[pl.ds(3 * width, width), at] = y1.astype(BF16)
            return carry

        lax.fori_loop(0, tiles, mixing, 0)

        def stage_two(j, carry):
            at = pl.ds(pl.multiple_of(j * tile, tile), tile)
            r0 = last(yg[: 3 * width], cols_of(own, 0, last, at))
            r1 = last(yg[width:], cols_of(own, 1, last, at))
            special = r0[:width] + r1[2 * width :]
            p00, p10 = r0[width : 2 * width], r0[2 * width :]
            p01, p11 = r1[:width], r1[width : 2 * width]
            plus, minus = p00 + p11, p00 - p11
            raw[4, :, at] = plus
            raw[5, :, at] = minus
            raw[6, :, at] = p01
            raw[7, :, at] = p10
            raw[8, :, at] = special
            edge = own_cut[mine, at].astype(F32)
            squares = tuple(
                c + jnp.sum(v * v) for c, v in zip(carry, (plus, minus, p01, p10, special))
            )
            return squares + (
                carry[5] + jnp.sum(special * edge),
                carry[6] + jnp.sum(plus * edge),
            )

        s_plus, s_minus, s_01, s_10, s_special, numer, denom = lax.fori_loop(
            0, tiles, stage_two, (zero,) * 7
        )
        sums[3] = s_plus
        sums[4] = s_minus
        sums[5] = s_01 + s_10
        sums[6] = s_special
        sums[7] = numer
        sums[8] = denom

    @pl.when(core == 0)
    def _():
        run(dot_nn, dot_nt, True)

    @pl.when(core != 0)
    def _():
        run(dot_nt, dot_nn, False)


def finish_kernel(scal, ints, raw, left, right):
    def one(out, base, order):
        for v, (index, coef) in enumerate(order):
            out[0, 0, v] = (raw[index] * scal[coef]).astype(BF16)

    @pl.when(ints[0] == 0)
    def _():
        one(left, 0, ((1, 0), (3, 1), (2, 1), (1, 2), (0, 3)))
        one(right, 0, ((4, 4), (6, 5), (7, 5), (5, 6), (8, 4)))

    @pl.when(ints[0] != 0)
    def _():
        one(left, 0, ((8, 4), (7, 5), (6, 5), (5, 6), (4, 4)))
        one(right, 0, ((0, 3), (2, 1), (3, 1), (1, 2), (1, 0)))


def body(mps, couplings, point_ids, site_group, field_levels, left_cut, right_cut):
    blocks = lax.axis_size("blk")
    points = lax.axis_size("pts")
    shards = lax.axis_size("bond")
    core = lax.axis_index("blk")
    here = lax.axis_index("pts")
    spot = lax.axis_index("bond")
    chi, width = mps.shape[1], mps.shape[3]
    part = chi // points
    rows, entries = width, 5 * chi * chi

    param_count = couplings.shape[0]
    chosen = (point_ids[0] == jnp.arange(param_count, dtype=jnp.int32)).astype(F32)
    params = jnp.sum(chosen[:, None] * couplings, axis=0)
    group_count = field_levels.shape[0]
    level = jnp.sum(
        jnp.where(site_group[0] == jnp.arange(group_count, dtype=jnp.int32), field_levels, 0.0)
    )
    level_other = swapped(jnp.broadcast_to(level, (8, 128)))[0, 0]
    half_xy, coupling_z, field = 0.5 * params[0], params[1], params[2]
    field_own, field_other = field * level, field * level_other

    tensor = jnp.transpose(mps[0], (1, 0, 2))
    flipped = jnp.transpose(mps[0], (1, 2, 0))
    cut = (jnp.where(core == 0, left_cut, right_cut) * SHRINK).astype(BF16)

    if points == 4 and shards == 4 and part == width:
        local, found = gather_pieces(tensor, cut)
        sources, plan = [], []
        for pieces, is_local in ((local, True), (found, False)):
            for piece, step, mask in pieces:
                sources.append(piece)
                plan.append((False, step, mask, is_local))
                sources.append(swapped(piece))
                plan.append((True, step, mask, is_local))
    else:
        full = lax.all_gather(tensor, "bond", axis=2, tiled=True)
        full_cut = lax.all_gather(cut, "bond", axis=0, tiled=True)
        sources = [full, full_cut, swapped(full), swapped(full_cut)]
        plan = [(False, None, 0, True), (False, None, 1, True), (True, None, 0, True), (True, None, 1, True)]

    ints = jnp.stack([core, here, spot]).astype(jnp.int32)
    scal = jnp.stack(
        [
            0.5 * field_other + 0.25 * coupling_z,
            0.5 * field_other - 0.25 * coupling_z,
            half_xy,
            0.5 * field_own,
        ]
    )
    smem = pl.BlockSpec(memory_space=pltpu.SMEM)
    vmem = pl.BlockSpec(memory_space=pltpu.VMEM)
    hbm = pl.BlockSpec(memory_space=pl.ANY)
    raw, sums = pl.pallas_call(
        functools.partial(energy_kernel, (chi, width, part, points, shards), tuple(plan)),
        out_shape=(
            jax.ShapeDtypeStruct((9, rows, chi), F32),
            jax.ShapeDtypeStruct((16,), F32),
        ),
        in_specs=[smem, smem, vmem] + [hbm] * len(sources),
        out_specs=(vmem, smem),
        scratch_shapes=[
            pltpu.VMEM((2, chi, chi), BF16),
            pltpu.VMEM((2, chi, chi), BF16),
            pltpu.VMEM((chi, chi), BF16),
            pltpu.VMEM((chi, chi), BF16),
            pltpu.VMEM((2 * rows, chi), BF16),
            pltpu.VMEM((2 * rows, chi), BF16),
            pltpu.VMEM((2 * rows, chi), BF16),
            pltpu.VMEM((4 * rows, chi), BF16),
            pltpu.VMEM((4 * rows, chi), BF16),
            pltpu.VMEM((4 * rows, chi), BF16),
            pltpu.SemaphoreType.DMA((3 * len(sources),)),
        ],
        compiler_params=pltpu.CompilerParams(vmem_limit_bytes=56 * 1024 * 1024),
        cost_estimate=pl.CostEstimate(
            flops=52 * rows * chi * chi, bytes_accessed=20 * chi * chi, transcendentals=0
        ),
        name="environments",
    )(scal, ints, flipped, *sources)

    one = jnp.ones((), F32)
    is_left = core == 0
    first_field = 0.5 * field_own
    xy_left, z_left = half_xy, 0.5 * coupling_z
    xy_first = jnp.where(is_left, xy_left, one)
    z_first = jnp.where(is_left, z_left, 0.5 * one)
    xy_second = jnp.where(is_left, one, xy_left)
    z_second = jnp.where(is_left, 0.5 * one, z_left)
    square_first = (
        sums[0] + (first_field**2 + z_first**2) * sums[1] + xy_first**2 * sums[2]
    )
    square_second = sums[3] + z_second**2 * sums[4] + xy_second**2 * sums[5] + sums[6]
    packed = jnp.stack([square_first, square_second, sums[7], sums[8]])
    packed = jnp.broadcast_to(jnp.pad(packed, (0, 4))[:, None], (8, 128))
    totals = bond_total(packed)
    across = swapped(totals)
    regrow = 1.0 / SHRINK

    def first_scale(total):
        return regrow * lax.rsqrt(total * (regrow * regrow) / entries + EPS)

    scale_one = first_scale(totals[0, 0])
    scale_mid = first_scale(across[0, 0])
    scale_two = scale_mid * lax.rsqrt(scale_mid * scale_mid * (totals[1, 0] / entries) + EPS)
    energy = jnp.where(is_left, across[2, 0] / across[3, 0], totals[2, 0] / totals[3, 0]) / blocks

    finals = jnp.stack(
        [
            scale_one * first_field,
            scale_one * xy_first,
            scale_one * z_first,
            scale_one,
            scale_two,
            scale_two * xy_second,
            scale_two * z_second,
        ]
    )
    band = min(rows, 64)
    out = jax.ShapeDtypeStruct((1, 1, 5, rows, chi), BF16)
    out_spec = pl.BlockSpec((1, 1, 5, band, chi), lambda i: (0, 0, 0, i, 0))
    left_env, right_env = pl.pallas_call(
        finish_kernel,
        grid=(rows // band,),
        out_shape=(out, out),
        in_specs=[smem, smem, pl.BlockSpec((9, band, chi), lambda i: (0, i, 0))],
        out_specs=(out_spec, out_spec),
        name="finish",
    )(finals, ints, raw)
    return left_env, right_env, energy[None]


def solution(mesh):
    placed = (
        P("blk", None, None, "bond"),
        P(),
        P("pts"),
        P("blk"),
        P(),
        P("bond", None),
        P("bond", None),
    )
    return jax.shard_map(
        body,
        mesh=mesh,
        in_specs=placed,
        out_specs=(
            P("blk", "pts", None, "bond", None),
            P("blk", "pts", None, "bond", None),
            P("pts"),
        ),
        check_vma=False,
    )
```

time: 682 us -> 173 us (0.25)
  waiting for transfers between devices: 306 us -> 65.6 us
  other arithmetic: 208 us -> 5.81 us
  local copies, waits for them, and re-layouts: 55.8 us -> 10.4 us
  Pallas kernels: 0 us -> 36.8 us
  blocking collectives: 30.8 us -> 0 us
  matrix products: 26.6 us -> 0 us
  starting transfers between devices: 28.8 us -> 36 us
    all_to_all x2 -> x0, waiting for transfers between devices: 230 us -> none  [cross(): lax.all_to_all(shortened(mixes[0]), 'bond', split_axis=3, concat_axis=2,...]
    convert_element_type x23 -> x2, other arithmetic: 158 us -> 1.55 us  [the longest x1 1.54 us: body(): cut = (jnp.where(core == 0, left_cut, right_cut) * SHRINK).astype(BF16)]
    all_gather x1 -> x0, waiting for transfers between devices: 70.1 us -> none  [body(): tensor = lax.all_gather(mps[0], 'bond', axis=2, tiled=True)]
    ppermute x4 -> x33, waiting for transfers between devices: 5.96 us -> 65.6 us  [the longest x12 47.1 us: crossed(): return lax.ppermute(value, axis, [(i, i ^ mask) for i in range(count)])]
    pallas_call x0 -> x2, Pallas kernels: none -> 36.8 us  [the longest x1 30.4 us: body(): pl.pallas_call(functools.partial(energy_kernel, (chi, width, part, points...]
    psum x3 -> x0, blocking collectives: 30.8 us -> none  [the longest x1 16.1 us: body(): lax.psum((numer * at_middle, denom * at_middle), ('blk', 'bond'))]
    another operation x8 -> x1, local copies, waits for them, and re-layouts: 27.8 us -> 0.69 us  [body(): jnp.stack([scale_one * first_field, scale_one * xy_first, scale_one * z_f...]
    dot_general x5 -> x0, matrix products: 26.6 us -> none  [the longest x1 7.41 us: bra_backward(): jnp.einsum('vtyz,qty->vzq', mixed_part, tensor, preferred_element_type=jn...]
  transfers between devices with their start and end apart: 7 -> 33, of which waited for: 5 -> 9; matrix products, arithmetic and copies ran while one was open for 2% -> 3% of each run, Pallas kernels for 0% -> 0%
where the time goes in v1:
time: 173 us; the launch traced here: 172 us
  waiting for transfers between devices  65.6 us (38%)
  Pallas kernels  36.8 us (21%)
  starting transfers between devices  36 us (21%)
  between operations  16.9 us (10%)
  local copies, waits for them, and re-layouts  10.4 us (6%)
  other arithmetic  5.81 us (3%)
    ppermute x12, waiting for transfers between devices, crossed(): return lax.ppermute(value, axis, [(i, i ^ mask) for i in range(count)])  47.1 us
    pallas_call x1, Pallas kernels, body(): pl.pallas_call(functools.partial(energy_kernel, (chi, width, part, points...  30.4 us
    ppermute x21, starting transfers between devices, shifted(): lax.ppermute(value, axis, [(i, (i + step) % count) for i in range(count)])  18.8 us
    ppermute x21, waiting for transfers between devices, shifted(): lax.ppermute(value, axis, [(i, (i + step) % count) for i in range(count)])  18.5 us
    ppermute x12, starting transfers between devices, crossed(): return lax.ppermute(value, axis, [(i, i ^ mask) for i in range(count)])  17.2 us
    pallas_call x1, Pallas kernels, body(): pl.pallas_call(finish_kernel, grid=(rows // band,), out_shape=(out, out),...  6.4 us
    unnamed x55, local copies, waits for them, and re-layouts  3.86 us
  transfers between devices with their start and end apart: 33, of which 9 were waited for; matrix products, arithmetic and copies ran while one was open for 3% of the time, Pallas kernels for 0%

profile of v1, /device:TPU:3, one launch (start us, length us, event | category | flops | bytes accessed | tf_op | source)
XLA Modules:
  0.0 171.5 jit_solution(9694961089301304489)
XLA Ops:
  0.6 1.5 multiply_convert_fusion
  2.3 1.5 copy.10
  4.1 0.6 copy-done
  5.1 0.9 fusion.7
  6.1 0.8 fusion.8
  7.2 1.3 collective-permute-start.5
  8.5 2.3 %collective-permute-start.13 = (bf16[768,256]{1,0:T(8,128)(2,1)S(1)}, bf16[768,256]{1,0:T(8,128)(2,1)S(1)}, u32[]{:S(2)}, u32[]{:S(2)}) collective-permute-start(bf16[768,256]{1,0:T(8,128)(2,1)S(1)} %fusion.3), channel_id=1, source_target_pairs={{0,2},{1,3},{2,0},{3,1},{4,6},{5,7},{6,4},{7,5},{8,10},{9,11},{10,... | collective-permute-start | bytes 1179656 | tf_op jit(solution)/shard_map/ppermute | solution.py:26
  10.8 1.1 collective-permute-start.21
  12.6 0.7 fusion.4
  13.2 0.7 broadcast_in_dim.18
  13.9 1.6 collective-permute-start
  15.6 0.7 collective-permute-done
  16.7 2.6 %collective-permute-done.5.refs_8_ = bf16[768,256]{1,0:T(8,128)(2,1)S(1)} collective-permute-done((bf16[768,256]{1,0:T(8,128)(2,1)S(1)}, bf16[768,256]{1,0:T(8,128)(2,1)S(1)}, u32[]{:S(2)}, u32[]{:S(2)}) %collective-permute-start.5) | collective-permute-done | bytes 393248 | tf_op jit(solution)/shard_map/ppermute | solution.py:26
  19.2 2.6 %collective-permute-start.3 = (bf16[768,256]{1,0:T(8,128)(2,1)S(1)}, bf16[768,256]{1,0:T(8,128)(2,1)S(1)}, u32[]{:S(2)}, u32[]{:S(2)}) collective-permute-start(bf16[768,256]{1,0:T(8,128)(2,1)S(1)} %get-tuple-element.22.refs_4_), channel_id=1, source_target_pairs={{0,16},{16,0},{1,17},{17,1},{2,18},{18,2},{3,19},{19,3},{4,20},{20... | collective-permute-start | bytes 1179656 | tf_op jit(solution)/shard_map/ppermute | solution.py:26
  21.8 15.2 %collective-permute-done.13.refs_16_ = bf16[768,256]{1,0:T(8,128)(2,1)S(1)} collective-permute-done((bf16[768,256]{1,0:T(8,128)(2,1)S(1)}, bf16[768,256]{1,0:T(8,128)(2,1)S(1)}, u32[]{:S(2)}, u32[]{:S(2)}) %collective-permute-start.13) | collective-permute-done | bytes 393248 | tf_op jit(solution)/shard_map/ppermute | solution.py:26
  37.0 0.6 collective-permute-start.4
  37.6 1.2 collective-permute-start.9
  39.1 1.2 collective-permute-start.15
  40.3 1.2 collective-permute-start.17
  41.7 14.9 %collective-permute-done.9.refs_12_ = bf16[768,256]{1,0:T(8,128)(2,1)S(1)} collective-permute-done((bf16[768,256]{1,0:T(8,128)(2,1)S(1)}, bf16[768,256]{1,0:T(8,128)(2,1)S(1)}, u32[]{:S(2)}, u32[]{:S(2)}) %collective-permute-start.9) | collective-permute-done | bytes 393248 | tf_op jit(solution)/shard_map/ppermute | solution.py:31
  56.9 1.2 collective-permute-start.25
  58.1 1.2 collective-permute-start.27
  59.3 14.3 %collective-permute-done.17.refs_20_ = bf16[768,256]{1,0:T(8,128)(2,1)S(1)} collective-permute-done((bf16[768,256]{1,0:T(8,128)(2,1)S(1)}, bf16[768,256]{1,0:T(8,128)(2,1)S(1)}, u32[]{:S(2)}, u32[]{:S(2)}) %collective-permute-start.17) | collective-permute-done | bytes 393248 | tf_op jit(solution)/shard_map/ppermute | solution.py:31
  73.8 1.7 collective-permute-start.14
  75.5 1.1 collective-permute-start.22
  76.6 13.8 %collective-permute-done.25.refs_28_ = bf16[768,256]{1,0:T(8,128)(2,1)} collective-permute-done((bf16[768,256]{1,0:T(8,128)(2,1)S(1)}, bf16[768,256]{1,0:T(8,128)(2,1)}, u32[]{:S(2)}, u32[]{:S(2)}) %collective-permute-start.25) | collective-permute-done | bytes 393248 | tf_op jit(solution)/shard_map/ppermute | solution.py:31
  90.4 0.9 collective-permute-start.6
  91.5 1.2 collective-permute-start.12
  92.8 0.7 copy-done.19
  93.5 0.7 copy-done.20
  94.9 0.6 collective-permute-start.20
  96.1 0.5 collective-permute-start.8
  97.0 0.6 fusion.14
  100.9 0.6 pad_add_fusion.ints
  101.5 0.5 slice.84
  103.3 0.6 pad_maximum_fusion.4.scal
  104.0 30.4 %environments.1 = (f32[9,256,1024]{2,1,0:T(8,128)}, f32[16]{0:T(128)}) custom-call(f32[4]{0:T(128)} %pad_maximum_fusion.4.scal, s32[3]{0:T(128)} %pad_add_fusion.ints, bf16[2,256,1024]{2,1,0:T(8,128)(2,1)} %bitcast.56, bf16[768,256]{1,0:T(8,128)(2,1)} %get-tuple-element.26.refs_0_, bf16[768,256]{1,0:T(8,128)(2,1)} %copy-done.10, ...), custom_call_target="tpu_custom_call" | custom-call | flops 13958643712 | bytes 20971520 | tf_op jit(solution)/shard_map/environments/pallas_call | solution.py:302
  134.4 1.6 fusion.13
  135.9 0.7 slice.102
  141.1 8.1 %collective-permute-start.29 = (f32[8,128]{1,0:T(8,128)S(1)}, f32[8,128]{1,0:T(8,128)S(1)}, u32[]{:S(2)}, u32[]{:S(2)}) collective-permute-start(f32[8,128]{1,0:T(8,128)S(1)} %broadcast_in_dim.19), channel_id=1, source_target_pairs={{0,1},{1,0},{2,3},{3,2},{4,5},{5,4},{6,7},{7,6},{8,9},{9,8},{10,11... | collective-permute-start | bytes 12296 | tf_op jit(solution)/shard_map/ppermute | solution.py:31
  149.2 1.8 %collective-permute-start.30 = (f32[8,128]{1,0:T(8,128)S(1)}, f32[8,128]{1,0:T(8,128)S(1)}, u32[]{:S(2)}, u32[]{:S(2)}) collective-permute-start(f32[8,128]{1,0:T(8,128)S(1)} %broadcast_in_dim.19), channel_id=1, source_target_pairs={{0,2},{1,3},{2,0},{3,1},{4,6},{5,7},{6,4},{7,5},{8,10},{9,11},{10,... | collective-permute-start | bytes 12296 | tf_op jit(solution)/shard_map/ppermute | solution.py:31
  151.3 1.2 collective-permute-done.30
  152.6 2.7 %collective-permute-done.31 = f32[8,128]{1,0:T(8,128)S(1)} collective-permute-done((f32[8,128]{1,0:T(8,128)S(1)}, f32[8,128]{1,0:T(8,128)S(1)}, u32[]{:S(2)}, u32[]{:S(2)}) %collective-permute-start.31) | collective-permute-done | bytes 4128 | tf_op jit(solution)/shard_map/ppermute | solution.py:31
  155.4 2.2 %collective-permute-start.32 = (f32[8,128]{1,0:T(8,128)S(1)}, f32[8,128]{1,0:T(8,128)S(1)}, u32[]{:S(2)}, u32[]{:S(2)}) collective-permute-start(f32[8,128]{1,0:T(8,128)S(1)} %add_add_fusion), channel_id=1, source_target_pairs={{0,16},{16,0},{1,17},{17,1},{2,18},{18,2},{3,19},{19,3},{4,20},{20... | collective-permute-start | bytes 12296 | tf_op jit(solution)/shard_map/ppermute | solution.py:26
  157.5 0.6 fusion.11
  160.1 0.5 fusion.12
  163.3 0.7 stack.97.scal
  164.0 6.4 %finish.1 = (bf16[1,1,5,256,1024]{4,3,2,1,0:T(8,128)(2,1)}, bf16[1,1,5,256,1024]{4,3,2,1,0:T(8,128)(2,1)}) custom-call(f32[7]{0:T(128)} %stack.97.scal, s32[3]{0:T(128)} %pad_add_fusion.ints, f32[9,256,1024]{2,1,0:T(8,128)} %get-tuple-element.8.raw), custom_call_target="tpu_custom_call" | custom-call | tf_op jit(solution)/shard_map/finish/pallas_call | solution.py:370
  (103 shorter events, 4.3 us)
Async XLA Ops:
  5.0 32.0 %copy-start.2 = (bf16[768,256]{1,0:T(8,128)(2,1)}, bf16[768,256]{1,0:T(8,128)(2,1)S(1)}, u32[]{:S(2)}) copy-start(bf16[768,256]{1,0:T(8,128)(2,1)S(1)} %get-tuple-element.20.refs_6_) | copy-start | bytes 1179652
  5.1 14.1 %copy-start.3 = (bf16[768,256]{1,0:T(8,128)(2,1)}, bf16[768,256]{1,0:T(8,128)(2,1)S(1)}, u32[]{:S(2)}) copy-start(bf16[768,256]{1,0:T(8,128)(2,1)S(1)} %get-tuple-element.22.refs_4_) | copy-start | bytes 1179652
  6.1 90.8 %copy-start.6 = (f32[64,3]{0,1:T(4,128)S(1)}, f32[64,3]{0,1:T(4,128)}, u32[]{:S(2)}) copy-start(f32[64,3]{0,1:T(4,128)} %param.8) | copy-start | bytes 2308
  7.2 12.1 %collective-permute-start.5 = (bf16[768,256]{1,0:T(8,128)(2,1)S(1)}, bf16[768,256]{1,0:T(8,128)(2,1)S(1)}, u32[]{:S(2)}, u32[]{:S(2)}) collective-permute-start(bf16[768,256]{1,0:T(8,128)(2,1)S(1)} %fusion.3), channel_id=1, source_target_pairs={{0,1},{1,2},{2,3},{3,0},{4,5},{5,6},{6,7},{7,4},{8,9},{9,10},{10,1... | collective-permute-start | bytes 1179656 | tf_op jit(solution)/shard_map/ppermute | solution.py:26
  8.5 28.5 %collective-permute-start.13 = (bf16[768,256]{1,0:T(8,128)(2,1)S(1)}, bf16[768,256]{1,0:T(8,128)(2,1)S(1)}, u32[]{:S(2)}, u32[]{:S(2)}) collective-permute-start(bf16[768,256]{1,0:T(8,128)(2,1)S(1)} %fusion.3), channel_id=1, source_target_pairs={{0,2},{1,3},{2,0},{3,1},{4,6},{5,7},{6,4},{7,5},{8,10},{9,11},{10,... | collective-permute-start | bytes 1179656 | tf_op jit(solution)/shard_map/ppermute | solution.py:26
  10.8 26.8 %collective-permute-start.21 = (bf16[768,256]{1,0:T(8,128)(2,1)S(1)}, bf16[768,256]{1,0:T(8,128)(2,1)S(1)}, u32[]{:S(2)}, u32[]{:S(2)}) collective-permute-start(bf16[768,256]{1,0:T(8,128)(2,1)S(1)} %fusion.3), channel_id=1, source_target_pairs={{0,3},{1,0},{2,1},{3,2},{4,7},{5,4},{6,5},{7,6},{8,11},{9,8},{10,9... | collective-permute-start | bytes 1179656 | tf_op jit(solution)/shard_map/ppermute | solution.py:26
  13.9 2.4 %collective-permute-start = (f32[8,128]{1,0:T(8,128)S(1)}, f32[8,128]{1,0:T(8,128)S(1)}, u32[]{:S(2)}, u32[]{:S(2)}) collective-permute-start(f32[8,128]{1,0:T(8,128)S(1)} %broadcast_in_dim.18), channel_id=1, source_target_pairs={{0,16},{16,0},{1,17},{17,1},{2,18},{18,2},{3,19},{19,3},{4,20},{20... | collective-permute-start | bytes 12296 | tf_op jit(solution)/shard_map/ppermute | solution.py:26
  15.5 23.4 %collective-permute-start.1 = (bf16[768,256]{1,0:T(8,128)(2,1)S(1)}, bf16[768,256]{1,0:T(8,128)(2,1)S(1)}, u32[]{:S(2)}, u32[]{:S(2)}) collective-permute-start(bf16[768,256]{1,0:T(8,128)(2,1)S(1)} %copy-done.5), channel_id=1, source_target_pairs={{0,16},{16,0},{1,17},{17,1},{2,18},{18,2},{3,19},{19,3},{4,20},{20... | collective-permute-start | bytes 1179656 | tf_op jit(solution)/shard_map/ppermute | solution.py:26
  16.3 22.7 %collective-permute-start.2 = (bf16[768,256]{1,0:T(8,128)(2,1)S(1)}, bf16[768,256]{1,0:T(8,128)(2,1)S(1)}, u32[]{:S(2)}, u32[]{:S(2)}) collective-permute-start(bf16[768,256]{1,0:T(8,128)(2,1)S(1)} %copy-done.4), channel_id=1, source_target_pairs={{0,16},{16,0},{1,17},{17,1},{2,18},{18,2},{3,19},{19,3},{4,20},{20... | collective-permute-start | bytes 1179656 | tf_op jit(solution)/shard_map/ppermute | solution.py:26
  19.2 84.7 %copy-start.7 = (bf16[768,256]{1,0:T(8,128)(2,1)}, bf16[768,256]{1,0:T(8,128)(2,1)S(1)}, u32[]{:S(2)}) copy-start(bf16[768,256]{1,0:T(8,128)(2,1)S(1)} %collective-permute-done.5.refs_8_) | copy-start | bytes 1179652
  19.2 21.0 %collective-permute-start.3 = (bf16[768,256]{1,0:T(8,128)(2,1)S(1)}, bf16[768,256]{1,0:T(8,128)(2,1)S(1)}, u32[]{:S(2)}, u32[]{:S(2)}) collective-permute-start(bf16[768,256]{1,0:T(8,128)(2,1)S(1)} %get-tuple-element.22.refs_4_), channel_id=1, source_target_pairs={{0,16},{16,0},{1,17},{17,1},{2,18},{18,2},{3,19},{19,3},{4,20},{20... | collective-permute-start | bytes 1179656 | tf_op jit(solution)/shard_map/ppermute | solution.py:26
  37.0 66.9 %copy-start.8 = (bf16[768,256]{1,0:T(8,128)(2,1)}, bf16[768,256]{1,0:T(8,128)(2,1)S(1)}, u32[]{:S(2)}) copy-start(bf16[768,256]{1,0:T(8,128)(2,1)S(1)} %collective-permute-done.13.refs_16_) | copy-start | bytes 1179652
  37.0 4.5 %collective-permute-start.4 = (bf16[768,256]{1,0:T(8,128)(2,1)S(1)}, bf16[768,256]{1,0:T(8,128)(2,1)S(1)}, u32[]{:S(2)}, u32[]{:S(2)}) collective-permute-start(bf16[768,256]{1,0:T(8,128)(2,1)S(1)} %get-tuple-element.20.refs_6_), channel_id=1, source_target_pairs={{0,16},{16,0},{1,17},{17,1},{2,18},{18,2},{3,19},{19,3},{4,20},{20... | collective-permute-start | bytes 1179656 | tf_op jit(solution)/shard_map/ppermute | solution.py:26
  37.6 66.3 %copy-start.9 = (bf16[768,256]{1,0:T(8,128)(2,1)}, bf16[768,256]{1,0:T(8,128)(2,1)S(1)}, u32[]{:S(2)}) copy-start(bf16[768,256]{1,0:T(8,128)(2,1)S(1)} %collective-permute-done.21.refs_24_) | copy-start | bytes 1179652
  37.6 19.0 %collective-permute-start.9 = (bf16[768,256]{1,0:T(8,128)(2,1)S(1)}, bf16[768,256]{1,0:T(8,128)(2,1)S(1)}, u32[]{:S(2)}, u32[]{:S(2)}) collective-permute-start(bf16[768,256]{1,0:T(8,128)(2,1)S(1)} %collective-permute-done.5.refs_8_), channel_id=1, source_target_pairs={{0,8},{4,12},{8,0},{12,4},{1,9},{5,13},{9,1},{13,5},{2,10},{6,14},... | collective-permute-start | bytes 1179656 | tf_op jit(solution)/shard_map/ppermute | solution.py:31
  38.9 53.9 %copy-start.10 = (bf16[768,256]{1,0:T(8,128)(2,1)}, bf16[768,256]{1,0:T(8,128)(2,1)S(1)}, u32[]{:S(2)}) copy-start(bf16[768,256]{1,0:T(8,128)(2,1)S(1)} %collective-permute-done.1.refs_1_) | copy-start | bytes 1179652
  38.9 18.0 %collective-permute-start.11 = (bf16[768,256]{1,0:T(8,128)(2,1)S(1)}, bf16[768,256]{1,0:T(8,128)(2,1)S(1)}, u32[]{:S(2)}, u32[]{:S(2)}) collective-permute-start(bf16[768,256]{1,0:T(8,128)(2,1)S(1)} %collective-permute-done.5.refs_8_), channel_id=1, source_target_pairs={{0,12},{4,8},{8,4},{12,0},{1,13},{5,9},{9,5},{13,1},{2,14},{6,10},... | collective-permute-start | bytes 1179656 | tf_op jit(solution)/shard_map/ppermute | solution.py:31
  39.1 53.7 %copy-start.11 = (bf16[768,256]{1,0:T(8,128)(2,1)}, bf16[768,256]{1,0:T(8,128)(2,1)S(1)}, u32[]{:S(2)}) copy-start(bf16[768,256]{1,0:T(8,128)(2,1)S(1)} %collective-permute-done.2.refs_3_) | copy-start | bytes 1179652
  39.1 19.1 %collective-permute-start.15 = (bf16[768,256]{1,0:T(8,128)(2,1)S(1)}, bf16[768,256]{1,0:T(8,128)(2,1)S(1)}, u32[]{:S(2)}, u32[]{:S(2)}) collective-permute-start(bf16[768,256]{1,0:T(8,128)(2,1)S(1)} %collective-permute-done.13.refs_16_), channel_id=1, source_target_pairs={{0,4},{4,0},{8,12},{12,8},{1,5},{5,1},{9,13},{13,9},{2,6},{6,2},{1... | collective-permute-start | bytes 1179656 | tf_op jit(solution)/shard_map/ppermute | solution.py:31
  40.3 52.5 %copy-start.12 = (bf16[768,256]{1,0:T(8,128)(2,1)}, bf16[768,256]{1,0:T(8,128)(2,1)S(1)}, u32[]{:S(2)}) copy-start(bf16[768,256]{1,0:T(8,128)(2,1)S(1)} %collective-permute-done.3.refs_5_) | copy-start | bytes 1179652
  40.3 33.3 %collective-permute-start.17 = (bf16[768,256]{1,0:T(8,128)(2,1)S(1)}, bf16[768,256]{1,0:T(8,128)(2,1)S(1)}, u32[]{:S(2)}, u32[]{:S(2)}) collective-permute-start(bf16[768,256]{1,0:T(8,128)(2,1)S(1)} %collective-permute-done.13.refs_16_), channel_id=1, source_target_pairs={{0,8},{4,12},{8,0},{12,4},{1,9},{5,13},{9,1},{13,5},{2,10},{6,14},... | collective-permute-start | bytes 1179656 | tf_op jit(solution)/shard_map/ppermute | solution.py:31
  41.5 51.3 %copy-start.13 = (bf16[768,256]{1,0:T(8,128)(2,1)}, bf16[768,256]{1,0:T(8,128)(2,1)S(1)}, u32[]{:S(2)}) copy-start(bf16[768,256]{1,0:T(8,128)(2,1)S(1)} %collective-permute-done.4.refs_7_) | copy-start | bytes 1179652
  41.5 32.3 %collective-permute-start.19 = (bf16[768,256]{1,0:T(8,128)(2,1)S(1)}, bf16[768,256]{1,0:T(8,128)(2,1)S(1)}, u32[]{:S(2)}, u32[]{:S(2)}) collective-permute-start(bf16[768,256]{1,0:T(8,128)(2,1)S(1)} %collective-permute-done.13.refs_16_), channel_id=1, source_target_pairs={{0,12},{4,8},{8,4},{12,0},{1,13},{5,9},{9,5},{13,1},{2,14},{6,10},... | collective-permute-start | bytes 1179656 | tf_op jit(solution)/shard_map/ppermute | solution.py:31
  56.6 39.5 %copy-start.14 = (bf16[768,256]{1,0:T(8,128)(2,1)}, bf16[768,256]{1,0:T(8,128)(2,1)S(1)}, u32[]{:S(2)}) copy-start(bf16[768,256]{1,0:T(8,128)(2,1)S(1)} %collective-permute-done.9.refs_12_) | copy-start | bytes 1179652
  56.6 18.9 %collective-permute-start.23 = (bf16[768,256]{1,0:T(8,128)(2,1)S(1)}, bf16[768,256]{1,0:T(8,128)(2,1)}, u32[]{:S(2)}, u32[]{:S(2)}) collective-permute-start(bf16[768,256]{1,0:T(8,128)(2,1)S(1)} %collective-permute-done.21.refs_24_), channel_id=1, source_target_pairs={{0,4},{4,0},{8,12},{12,8},{1,5},{5,1},{9,13},{13,9},{2,6},{6,2},{1... | collective-permute-start | bytes 1179656 | tf_op jit(solution)/shard_map/ppermute | solution.py:31
  56.9 47.1 %copy-start.15 = (bf16[768,256]{1,0:T(8,128)(2,1)}, bf16[768,256]{1,0:T(8,128)(2,1)S(1)}, u32[]{:S(2)}) copy-start(bf16[768,256]{1,0:T(8,128)(2,1)S(1)} %collective-permute-done.11.refs_14_) | copy-start | bytes 1179652
  56.9 33.5 %collective-permute-start.25 = (bf16[768,256]{1,0:T(8,128)(2,1)S(1)}, bf16[768,256]{1,0:T(8,128)(2,1)}, u32[]{:S(2)}, u32[]{:S(2)}) collective-permute-start(bf16[768,256]{1,0:T(8,128)(2,1)S(1)} %collective-permute-done.21.refs_24_), channel_id=1, source_target_pairs={{0,8},{4,12},{8,0},{12,4},{1,9},{5,13},{9,1},{13,5},{2,10},{6,14},... | collective-permute-start | bytes 1179656 | tf_op jit(solution)/shard_map/ppermute | solution.py:31
  58.1 45.8 %copy-start.16 = (bf16[768,256]{1,0:T(8,128)(2,1)}, bf16[768,256]{1,0:T(8,128)(2,1)S(1)}, u32[]{:S(2)}) copy-start(bf16[768,256]{1,0:T(8,128)(2,1)S(1)} %collective-permute-done.15.refs_18_) | copy-start | bytes 1179652
  58.1 33.2 %collective-permute-start.27 = (bf16[768,256]{1,0:T(8,128)(2,1)S(1)}, bf16[768,256]{1,0:T(8,128)(2,1)}, u32[]{:S(2)}, u32[]{:S(2)}) collective-permute-start(bf16[768,256]{1,0:T(8,128)(2,1)S(1)} %collective-permute-done.21.refs_24_), channel_id=1, source_target_pairs={{0,12},{4,8},{8,4},{12,0},{1,13},{5,9},{9,5},{13,1},{2,14},{6,10},... | collective-permute-start | bytes 1179656 | tf_op jit(solution)/shard_map/ppermute | solution.py:31
  73.6 30.4 %copy-start.17 = (bf16[768,256]{1,0:T(8,128)(2,1)}, bf16[768,256]{1,0:T(8,128)(2,1)S(1)}, u32[]{:S(2)}) copy-start(bf16[768,256]{1,0:T(8,128)(2,1)S(1)} %collective-permute-done.17.refs_20_) | copy-start | bytes 1179652
  73.6 17.9 %collective-permute-start.7 = (bf16[768,256]{1,0:T(8,128)(2,1)S(1)}, bf16[768,256]{1,0:T(8,128)(2,1)}, u32[]{:S(2)}, u32[]{:S(2)}) collective-permute-start(bf16[768,256]{1,0:T(8,128)(2,1)S(1)} %collective-permute-done.5.refs_8_), channel_id=1, source_target_pairs={{0,4},{4,0},{8,12},{12,8},{1,5},{5,1},{9,13},{13,9},{2,6},{6,2},{1... | collective-permute-start | bytes 1179656 | tf_op jit(solution)/shard_map/ppermute | solution.py:31
  73.8 30.1 %copy-start.18 = (bf16[768,256]{1,0:T(8,128)(2,1)}, bf16[768,256]{1,0:T(8,128)(2,1)S(1)}, u32[]{:S(2)}) copy-start(bf16[768,256]{1,0:T(8,128)(2,1)S(1)} %collective-permute-done.19.refs_22_) | copy-start | bytes 1179652
  73.8 18.9 %collective-permute-start.14 = (bf16[768,256]{1,0:T(8,128)(2,1)S(1)}, bf16[768,256]{1,0:T(8,128)(2,1)S(1)}, u32[]{:S(2)}, u32[]{:S(2)}) collective-permute-start(bf16[768,256]{1,0:T(8,128)(2,1)S(1)} %collective-permute-done.13.refs_16_), channel_id=1, source_target_pairs={{0,16},{16,0},{1,17},{17,1},{2,18},{18,2},{3,19},{19,3},{4,20},{20... | collective-permute-start | bytes 1179656 | tf_op jit(solution)/shard_map/ppermute | solution.py:26
  75.5 17.3 %collective-permute-start.22 = (bf16[768,256]{1,0:T(8,128)(2,1)S(1)}, bf16[768,256]{1,0:T(8,128)(2,1)S(1)}, u32[]{:S(2)}, u32[]{:S(2)}) collective-permute-start(bf16[768,256]{1,0:T(8,128)(2,1)S(1)} %collective-permute-done.21.refs_24_), channel_id=1, source_target_pairs={{0,16},{16,0},{1,17},{17,1},{2,18},{18,2},{3,19},{19,3},{4,20},{20... | collective-permute-start | bytes 1179656 | tf_op jit(solution)/shard_map/ppermute | solution.py:26
  90.4 4.4 %collective-permute-start.6 = (bf16[768,256]{1,0:T(8,128)(2,1)S(1)}, bf16[768,256]{1,0:T(8,128)(2,1)S(1)}, u32[]{:S(2)}, u32[]{:S(2)}) collective-permute-start(bf16[768,256]{1,0:T(8,128)(2,1)S(1)} %collective-permute-done.5.refs_8_), channel_id=1, source_target_pairs={{0,16},{16,0},{1,17},{17,1},{2,18},{18,2},{3,19},{19,3},{4,20},{20... | collective-permute-start | bytes 1179656 | tf_op jit(solution)/shard_map/ppermute | solution.py:26
  91.4 4.1 %collective-permute-start.10 = (bf16[768,256]{1,0:T(8,128)(2,1)S(1)}, bf16[768,256]{1,0:T(8,128)(2,1)S(1)}, u32[]{:S(2)}, u32[]{:S(2)}) collective-permute-start(bf16[768,256]{1,0:T(8,128)(2,1)S(1)} %collective-permute-done.9.refs_12_), channel_id=1, source_target_pairs={{0,16},{16,0},{1,17},{17,1},{2,18},{18,2},{3,19},{19,3},{4,20},{20... | collective-permute-start | bytes 1179656 | tf_op jit(solution)/shard_map/ppermute | solution.py:26
  91.5 4.1 %collective-permute-start.12 = (bf16[768,256]{1,0:T(8,128)(2,1)S(1)}, bf16[768,256]{1,0:T(8,128)(2,1)S(1)}, u32[]{:S(2)}, u32[]{:S(2)}) collective-permute-start(bf16[768,256]{1,0:T(8,128)(2,1)S(1)} %collective-permute-done.11.refs_14_), channel_id=1, source_target_pairs={{0,16},{16,0},{1,17},{17,1},{2,18},{18,2},{3,19},{19,3},{4,20},{20... | collective-permute-start | bytes 1179656 | tf_op jit(solution)/shard_map/ppermute | solution.py:26
  92.7 3.3 %collective-permute-start.16 = (bf16[768,256]{1,0:T(8,128)(2,1)S(1)}, bf16[768,256]{1,0:T(8,128)(2,1)S(1)}, u32[]{:S(2)}, u32[]{:S(2)}) collective-permute-start(bf16[768,256]{1,0:T(8,128)(2,1)S(1)} %collective-permute-done.15.refs_18_), channel_id=1, source_target_pairs={{0,16},{16,0},{1,17},{17,1},{2,18},{18,2},{3,19},{19,3},{4,20},{20... | collective-permute-start | bytes 1179656 | tf_op jit(solution)/shard_map/ppermute | solution.py:26
  94.2 1.9 %collective-permute-start.18 = (bf16[768,256]{1,0:T(8,128)(2,1)S(1)}, bf16[768,256]{1,0:T(8,128)(2,1)S(1)}, u32[]{:S(2)}, u32[]{:S(2)}) collective-permute-start(bf16[768,256]{1,0:T(8,128)(2,1)S(1)} %collective-permute-done.17.refs_20_), channel_id=1, source_target_pairs={{0,16},{16,0},{1,17},{17,1},{2,18},{18,2},{3,19},{19,3},{4,20},{20... | collective-permute-start | bytes 1179656 | tf_op jit(solution)/shard_map/ppermute | solution.py:26
  94.9 9.0 %collective-permute-start.20 = (bf16[768,256]{1,0:T(8,128)(2,1)S(1)}, bf16[768,256]{1,0:T(8,128)(2,1)}, u32[]{:S(2)}, u32[]{:S(2)}) collective-permute-start(bf16[768,256]{1,0:T(8,128)(2,1)S(1)} %collective-permute-done.19.refs_22_), channel_id=1, source_target_pairs={{0,16},{16,0},{1,17},{17,1},{2,18},{18,2},{3,19},{19,3},{4,20},{20... | collective-permute-start | bytes 1179656 | tf_op jit(solution)/shard_map/ppermute | solution.py:26
  95.5 8.4 %collective-permute-start.24 = (bf16[768,256]{1,0:T(8,128)(2,1)}, bf16[768,256]{1,0:T(8,128)(2,1)}, u32[]{:S(2)}, u32[]{:S(2)}) collective-permute-start(bf16[768,256]{1,0:T(8,128)(2,1)} %collective-permute-done.23.refs_26_), channel_id=1, source_target_pairs={{0,16},{16,0},{1,17},{17,1},{2,18},{18,2},{3,19},{19,3},{4,20},{20... | collective-permute-start | bytes 1179656 | tf_op jit(solution)/shard_map/ppermute | solution.py:26
  95.6 8.3 %collective-permute-start.26 = (bf16[768,256]{1,0:T(8,128)(2,1)}, bf16[768,256]{1,0:T(8,128)(2,1)}, u32[]{:S(2)}, u32[]{:S(2)}) collective-permute-start(bf16[768,256]{1,0:T(8,128)(2,1)} %collective-permute-done.25.refs_28_), channel_id=1, source_target_pairs={{0,16},{16,0},{1,17},{17,1},{2,18},{18,2},{3,19},{19,3},{4,20},{20... | collective-permute-start | bytes 1179656 | tf_op jit(solution)/shard_map/ppermute | solution.py:26
  96.0 7.9 %collective-permute-start.28 = (bf16[768,256]{1,0:T(8,128)(2,1)}, bf16[768,256]{1,0:T(8,128)(2,1)}, u32[]{:S(2)}, u32[]{:S(2)}) collective-permute-start(bf16[768,256]{1,0:T(8,128)(2,1)} %collective-permute-done.27.refs_30_), channel_id=1, source_target_pairs={{0,16},{16,0},{1,17},{17,1},{2,18},{18,2},{3,19},{19,3},{4,20},{20... | collective-permute-start | bytes 1179656 | tf_op jit(solution)/shard_map/ppermute | solution.py:26
  96.1 7.8 %collective-permute-start.8 = (bf16[768,256]{1,0:T(8,128)(2,1)}, bf16[768,256]{1,0:T(8,128)(2,1)}, u32[]{:S(2)}, u32[]{:S(2)}) collective-permute-start(bf16[768,256]{1,0:T(8,128)(2,1)} %collective-permute-done.7.refs_10_), channel_id=1, source_target_pairs={{0,16},{16,0},{1,17},{17,1},{2,18},{18,2},{3,19},{19,3},{4,20},{20... | collective-permute-start | bytes 1179656 | tf_op jit(solution)/shard_map/ppermute | solution.py:26
  141.1 10.2 %collective-permute-start.29 = (f32[8,128]{1,0:T(8,128)S(1)}, f32[8,128]{1,0:T(8,128)S(1)}, u32[]{:S(2)}, u32[]{:S(2)}) collective-permute-start(f32[8,128]{1,0:T(8,128)S(1)} %broadcast_in_dim.19), channel_id=1, source_target_pairs={{0,1},{1,0},{2,3},{3,2},{4,5},{5,4},{6,7},{7,6},{8,9},{9,8},{10,11... | collective-permute-start | bytes 12296 | tf_op jit(solution)/shard_map/ppermute | solution.py:31
  149.2 3.4 %collective-permute-start.30 = (f32[8,128]{1,0:T(8,128)S(1)}, f32[8,128]{1,0:T(8,128)S(1)}, u32[]{:S(2)}, u32[]{:S(2)}) collective-permute-start(f32[8,128]{1,0:T(8,128)S(1)} %broadcast_in_dim.19), channel_id=1, source_target_pairs={{0,2},{1,3},{2,0},{3,1},{4,6},{5,7},{6,4},{7,5},{8,10},{9,11},{10,... | collective-permute-start | bytes 12296 | tf_op jit(solution)/shard_map/ppermute | solution.py:31
  151.0 4.3 %collective-permute-start.31 = (f32[8,128]{1,0:T(8,128)S(1)}, f32[8,128]{1,0:T(8,128)S(1)}, u32[]{:S(2)}, u32[]{:S(2)}) collective-permute-start(f32[8,128]{1,0:T(8,128)S(1)} %broadcast_in_dim.19), channel_id=1, source_target_pairs={{0,3},{1,2},{2,1},{3,0},{4,7},{5,6},{6,5},{7,4},{8,11},{9,10},{10,... | collective-permute-start | bytes 12296 | tf_op jit(solution)/shard_map/ppermute | solution.py:31
  155.4 4.7 %collective-permute-start.32 = (f32[8,128]{1,0:T(8,128)S(1)}, f32[8,128]{1,0:T(8,128)S(1)}, u32[]{:S(2)}, u32[]{:S(2)}) collective-permute-start(f32[8,128]{1,0:T(8,128)S(1)} %add_add_fusion), channel_id=1, source_target_pairs={{0,16},{16,0},{1,17},{17,1},{2,18},{18,2},{3,19},{19,3},{4,20},{20... | collective-permute-start | bytes 12296 | tf_op jit(solution)/shard_map/ppermute | solution.py:26
  (12 other events, 34.8 us)
